TPU v7x, 32 devices: a whole 2x2x4 slice. The times are simulated.
32 devices in a mesh: bank: 4 (over x, core), lane: 8 (over z, y).
Axes of the slice: x: 2, y: 2, z: 4, core: 2. Of those that a mesh axis runs over, the one named last changes fastest.
Arguments:
- amplitudes: float32 [2, 512, 128, 128], P(None, ('bank', 'lane')), may hold values from -6 to 6
- energies: float32 [512, 128, 128], P(('bank', 'lane')), may hold values from -2 to 2
- diagonal_angles: float32 [2, 128], replicated, may hold values from 0.3 to 1.2
- turn_angles: float32 [2, 4], replicated, may hold values from 0.3 to 1.2
Outputs:
- state_after: float32 [2, 512, 128, 128], P(None, ('bank', 'lane'))
All inputs are finite; a program needn't handle non-finite values.
Results may differ from a plain program's by a relative error of at most 0.0003.
Values sent between devices are 32-bit elements; how exact they have to be, the bound alone decides.
A program may use at most 64 MiB of HBM per device.

v0:
```python
import functools
import math

import jax
import jax.numpy as jnp
from jax import lax
from jax.experimental import pallas as pl
from jax.experimental.pallas import tpu as pltpu
from jax.sharding import PartitionSpec as P

LAYERS = 2
VMEM_MOST = 67043328
ROOM = 1 << 18
MESH = pl.DeviceIdType.MESH
SUB = 8
ROWS_SLAB = 16


def bits_of(count):
    return count.bit_length() - 1


def xor(number, mask, count):
    out = 0
    for place in range(bits_of(count)):
        weight = 1 << place
        one = lax.rem(lax.div(number, weight), 2) + lax.rem(lax.div(mask, weight), 2)
        out = out + lax.rem(one, 2) * weight
    return out


def flips(number, count):
    out = [number]
    for place in range(bits_of(count)):
        weight = 1 << place
        change = weight - 2 * weight * lax.rem(lax.div(number, weight), 2)
        out = out + [other + change for other in out]
    return out


def cos_sin(turn):
    half = 0.5 * turn
    square = half * half
    sine = jnp.full_like(half, -1.0 / math.factorial(11))
    for power in (9, 7, 5, 3, 1):
        sine = sine * square + (-1.0) ** (power // 2) / math.factorial(power)
    sine = sine * half
    cosine = jnp.full_like(half, -1.0 / math.factorial(10))
    for power in (8, 6, 4, 2, 0):
        cosine = cosine * square + (-1.0) ** (power // 2) / math.factorial(power)
    double = sine + sine
    return 1.0 - double * sine, double * cosine


def turned(pieces, slope, low, high):
    pieces = list(pieces)
    for place in range(low, high):
        step = 1 << place
        for at in range(len(pieces)):
            if not at & step:
                u, v = pieces[at], pieces[at + step]
                pieces[at], pieces[at + step] = u - slope * v, v + slope * u
    return pieces


def mix_slabs(values, mixed, tangent):
    slabs, rows, _ = values.shape
    places = [(s, slice(e, e + SUB)) for s in range(slabs) for e in range(0, rows, SUB)]
    pieces = [values[s, e, :] for s, e in places]
    pieces = turned(pieces, tangent, 0, bits_of(len(places)))
    for (s, e), piece in zip(places, pieces):
        mixed[s, e, :] = piece


def finish(values, tangent, out_hbm, mixed, sem):
    _, blocks, groups, _, _, _ = values.shape

    def one(b, carry):
        for part in range(2):
            for g in range(groups):
                mix_slabs(values.at[part, b, g], mixed.at[part, b, g], tangent[...])
        pltpu.make_async_copy(mixed.at[:, b], out_hbm.at[:, b], sem).start()
        return carry

    lax.fori_loop(0, blocks, one, 0)
    pltpu.make_async_copy(mixed, out_hbm, sem).wait()


def kernel(
    nb, nl, amp_hbm, en_hbm, diag_hbm, turn_hbm, out, last,
    amp, en, diag_ref, turn_ref, rs, re, back, table, slope, signed,
    in_sem, s_send, s_recv, e_send, e_recv, b_send, b_recv,
):
    _, blocks, groups, slabs, rows, lanes = amp.shape
    devices = nb * nl
    others = devices - 1
    eights = rows // SUB
    me_b, me_l = lax.axis_index("bank"), lax.axis_index("lane")
    me = me_b * nl + me_l
    my_block, my_group = lax.rem(me, blocks), lax.div(me, blocks)

    load_en = pltpu.make_async_copy(en_hbm, en, in_sem.at[0])
    load_en.start()
    load_turn = pltpu.make_async_copy(turn_hbm, turn_ref, in_sem.at[2])
    load_turn.start()
    load_diag = pltpu.make_async_copy(diag_hbm, diag_ref, in_sem.at[3])
    load_diag.start()
    load_amp = pltpu.make_async_copy(amp_hbm, amp, in_sem.at[1])
    load_amp.start()

    def peer(k):
        db = xor(me_b, lax.rem(k, nb), nb)
        dl = lax.rem(me_l + lax.div(k, nb), nl)
        return db, dl

    flip_b = flips(me_b, nb)
    flip_l = flips(me_l, nl)

    def to_peers_at_once(order, action):
        for k in order:
            db, dl = flip_b[k % nb], flip_l[k // nb]
            action(db, dl, db * nl + dl)

    def to_peers(action):
        def step(k, carry):
            db, dl = peer(k)
            action(db, dl, db * nl + dl)
            return carry

        lax.fori_loop(1, devices, step, 0)

    barrier = pltpu.get_barrier_semaphore()
    to_peers_at_once(
        range(others, 0, -1),
        lambda db, dl, d: pl.semaphore_signal(
            barrier, inc=1, device_id=(db, dl), device_id_type=MESH
        ),
    )
    pl.semaphore_wait(barrier, others)

    def send_en(low, count, at, each=to_peers):
        def one(db, dl, d):
            pltpu.make_async_remote_copy(
                src_ref=en.at[lax.rem(d, blocks), lax.div(d, blocks), pl.ds(low, count)],
                dst_ref=re.at[me, pl.ds(low, count)],
                send_sem=e_send.at[at],
                recv_sem=e_recv.at[at],
                device_id=(db, dl),
                device_id_type=MESH,
            ).start()

        each(one)

    def send_state(s):
        def one(db, dl, d):
            pltpu.make_async_remote_copy(
                src_ref=amp.at[:, lax.rem(d, blocks), lax.div(d, blocks), s],
                dst_ref=rs.at[me, :, s],
                send_sem=s_send.at[s],
                recv_sem=s_recv.at[s],
                device_id=(db, dl),
                device_id_type=MESH,
            ).start()

        to_peers(one)

    def send_back(s):
        def one(db, dl, d):
            pltpu.make_async_remote_copy(
                src_ref=rs.at[d, :, s],
                dst_ref=back.at[:, my_block, my_group, s],
                send_sem=b_send.at[s],
                recv_sem=b_recv.at[s],
                device_id=(db, dl),
                device_id_type=MESH,
            ).start()

        to_peers(one)

    def wait_en(sem, low, count):
        whole = re.at[pl.ds(0, others), pl.ds(low, count)]
        pltpu.make_async_copy(whole, whole, sem).wait()

    def wait_state(sem, s):
        whole = rs.at[pl.ds(0, others), :, s]
        pltpu.make_async_copy(whole, whole, sem).wait()

    load_en.wait()
    send_en(0, 1, 0, functools.partial(to_peers_at_once, range(1, devices)))

    load_turn.wait()
    load_diag.wait()
    scales = []
    for layer in range(LAYERS):
        cosines = []
        for group in range(4):
            angle = jnp.broadcast_to(turn_ref[layer : layer + 1, group : group + 1], (SUB, lanes))
            cosine, sine = cos_sin(angle)
            cosines.append(cosine)
            slope[layer, group] = sine / cosine
        sublane = lax.broadcasted_iota(jnp.int32, (SUB, lanes), 0)
        for place in range(3):
            sign = ((sublane >> place) & 1) * 2 - 1
            signed[layer, place] = slope[layer, 1] * sign.astype(jnp.float32)
        scale = jnp.ones((SUB, lanes), jnp.float32)
        for group, count in ((0, lanes), (1, groups * slabs * rows), (2, blocks * nb), (3, nl)):
            for _ in range(bits_of(count)):
                scale = scale * cosines[group]
        scales.append(scale[0:1, :])
    last[...] = slope[LAYERS - 1, 1]

    def build_table(layer):
        here = lax.broadcasted_iota(jnp.int32, (lanes, lanes), 0)
        there = lax.broadcasted_iota(jnp.int32, (lanes, lanes), 1)
        whole = jnp.broadcast_to(scales[layer], (lanes, lanes))
        tangent = jnp.broadcast_to(slope[layer, 0, 0:1, :], (lanes, lanes))
        for place in range(bits_of(lanes)):
            source, target = (here >> place) & 1, (there >> place) & 1
            sign = (target - source).astype(jnp.float32)
            whole = whole * jnp.where(source == target, 1.0, sign * tangent)
        high = whole.astype(jnp.bfloat16)
        low = (whole - high.astype(jnp.float32)).astype(jnp.bfloat16)
        table[layer, :lanes, :lanes] = high
        table[layer, lanes:, :lanes] = high
        table[layer, :lanes, lanes:] = low
        table[layer, lanes:, lanes:] = jnp.zeros_like(low)

    def over(count, action):
        def step(i, carry):
            action(i)
            return carry

        lax.fori_loop(0, count, step, 0)

    def at_eight(i):
        return pl.ds(pl.multiple_of(i * SUB, SUB), SUB)

    load_amp.wait()
    first_angle = jnp.broadcast_to(diag_ref[0:1, :], (rows, lanes))

    def mix_home(values, mixed, layer, s):
        def one(i):
            part, eight = lax.div(i, eights), at_eight(lax.rem(i, eights))
            pieces = [
                values[part, b, g, s, eight, :] for g in range(groups) for b in range(blocks)
            ]
            inner = bits_of(blocks)
            pieces = turned(pieces, slope[layer, 2], 0, inner)
            pieces = turned(pieces, slope[layer, 1], inner, inner + bits_of(groups))
            for at, piece in enumerate(pieces):
                mixed[part, at % blocks, at // blocks, s, eight, :] = piece

        over(2 * eights, one)

    for s in range(slabs):

        def phase_home(b):
            for g in range(groups):
                cosine, sine = cos_sin(first_angle * en[b, g, s])
                real, imag = amp[0, b, g, s], amp[1, b, g, s]
                amp[0, b, g, s] = real * cosine + imag * sine
                amp[1, b, g, s] = imag * cosine - real * sine

        over(blocks, phase_home)
        mix_home(amp, amp, 0, s)
        send_state(s)
    if slabs > 1:
        send_en(1, slabs - 1, 1)
    for part in range(2):
        rs[me, part] = amp[part, my_block, my_group]
    re[me] = en[my_block, my_group]
    for layer in range(LAYERS):
        build_table(layer)

    batch = 8

    def mix_lanes(layer, s):
        def one(i):
            at = pl.ds(i * batch, batch)
            values = rs[at, :, s].reshape(batch * 2 * rows, lanes)
            high = values.astype(jnp.bfloat16)
            low = (values - high.astype(jnp.float32)).astype(jnp.bfloat16)
            both = jnp.dot(
                jnp.concatenate([high, low], axis=1),
                table[layer],
                preferred_element_type=jnp.float32,
            )
            both = both[:, :lanes] + both[:, lanes:]
            rs[at, :, s] = both.reshape(batch, 2, rows, lanes)

        over(devices // batch, one)

    def mix_devices(layer, s):
        def one(part):
            for eight in range(eights):
                pieces = []
                for d in range(devices):
                    piece = rs[d, part, s, eight * SUB : (eight + 1) * SUB, :]
                    sublane = lax.broadcasted_iota(jnp.int32, (SUB, lanes), 0)
                    for place in range(3):
                        step = 1 << place
                        other = pltpu.roll(piece, step, 0)
                        if place < 2:
                            back_roll = pltpu.roll(piece, SUB - step, 0)
                            other = jnp.where((sublane >> place) & 1 == 1, other, back_roll)
                        piece = piece + signed[layer, place] * other
                    pieces.append(piece)
                inner = bits_of(nl)
                pieces = turned(pieces, slope[layer, 3], 0, inner)
                pieces = turned(pieces, slope[layer, 2], inner, inner + bits_of(nb))
                for d in range(devices):
                    rs[d, part, s, eight * SUB : (eight + 1) * SUB, :] = pieces[d]

        over(2, one)

    for s in range(slabs):
        wait_state(s_recv.at[s], s)
        mix_lanes(0, s)
        mix_devices(0, s)

    def slabs_away(d):
        for part in range(2):
            mix_slabs(rs.at[d, part], rs.at[d, part], slope[0, 1])

    over(devices, slabs_away)

    second_angle = jnp.broadcast_to(diag_ref[1:2, :], (rows, lanes))
    for s in range(slabs):
        if s == 0:
            wait_en(e_recv.at[0], 0, 1)
        if s == 1:
            wait_en(e_recv.at[1], 1, slabs - 1)

        def phase_away(d):
            cosine, sine = cos_sin(second_angle * re[d, s])
            real, imag = rs[d, 0, s], rs[d, 1, s]
            rs[d, 0, s] = real * cosine + imag * sine
            rs[d, 1, s] = imag * cosine - real * sine

        over(devices, phase_away)
        mix_lanes(1, s)
        mix_devices(1, s)
        send_back(s)
    for part in range(2):
        back[part, my_block, my_group] = rs[me, part]

    for s in range(slabs):
        wait_state(b_recv.at[s], s)
        mix_home(back, out, 1, s)

    wait_en(e_send.at[0], 0, 1)
    if slabs > 1:
        wait_en(e_send.at[1], 1, slabs - 1)
    for s in range(slabs):
        wait_state(s_send.at[s], s)
        wait_state(b_send.at[s], s)


def body(nb, nl, amplitudes, energies, diagonal_angles, turn_angles):
    _, blocks, all_rows, lanes = amplitudes.shape
    devices = nb * nl
    groups = devices // blocks
    rows = ROWS_SLAB
    slabs = all_rows // (groups * rows)
    home = (2, blocks, groups, slabs, rows, lanes)
    away = (devices, 2, slabs, rows, lanes)
    grant = VMEM_MOST - 4 * amplitudes.size - ROOM
    dma = pltpu.SemaphoreType.DMA
    hbm = pl.BlockSpec(memory_space=pl.ANY)
    vmem = pl.BlockSpec(memory_space=pltpu.VMEM)
    values, tangent = pl.pallas_call(
        functools.partial(kernel, nb, nl),
        out_shape=[pltpu.VMEM(home, jnp.float32), pltpu.VMEM((SUB, lanes), jnp.float32)],
        in_specs=[hbm] * 4,
        out_specs=[vmem, vmem],
        scratch_shapes=[
            pltpu.VMEM(home, jnp.float32),
            pltpu.VMEM(home[1:], jnp.float32),
            pltpu.VMEM(diagonal_angles.shape, jnp.float32),
            pltpu.VMEM(turn_angles.shape, jnp.float32),
            pltpu.VMEM(away, jnp.float32),
            pltpu.VMEM((devices,) + away[2:], jnp.float32),
            pltpu.VMEM(home, jnp.float32),
            pltpu.VMEM((LAYERS, 2 * lanes, 2 * lanes), jnp.bfloat16),
            pltpu.VMEM((LAYERS, 4, SUB, lanes), jnp.float32),
            pltpu.VMEM((LAYERS, 3, SUB, lanes), jnp.float32),
            dma((4,)),
            dma((slabs,)),
            dma((slabs,)),
            dma((2,)),
            dma((2,)),
            dma((slabs,)),
            dma((slabs,)),
        ],
        compiler_params=pltpu.CompilerParams(
            collective_id=0, has_side_effects=True, vmem_limit_bytes=grant
        ),
    )(amplitudes.reshape(home), energies.reshape(home[1:]), diagonal_angles, turn_angles)
    out = pl.pallas_call(
        finish,
        out_shape=jax.ShapeDtypeStruct(home, jnp.float32),
        in_specs=[vmem, vmem],
        out_specs=hbm,
        scratch_shapes=[pltpu.VMEM(home, jnp.float32), dma],
        compiler_params=pltpu.CompilerParams(vmem_limit_bytes=32 * 1024 * 1024),
    )(values, tangent)
    return out.reshape(amplitudes.shape)


def solution(mesh):
    placed = (P(None, ("bank", "lane"), None, None), P(("bank", "lane"), None, None), P(), P())
    return jax.shard_map(
        functools.partial(body, mesh.shape["bank"], mesh.shape["lane"]),
        mesh=mesh,
        in_specs=placed,
        out_specs=P(None, ("bank", "lane"), None, None),
        check_vma=False,
    )
```

profile of v0, /device:TPU:9, one launch (start us, length us, event | category | flops | bytes accessed | tf_op | source)
XLA Modules:
  0.0 119.7 jit_solution(10077174601747719656)
XLA Ops:
  0.0 118.3 %shard_map.46 = (f32[2,16,2,4,16,128]{5,4,3,2,1,0:T(8,128)S(1)}, f32[8,128]{1,0:T(8,128)S(1)}) custom-call(f32[2,16,2,4,16,128]{5,4,3,2,1,0:T(8,128)} %bitcast.3, f32[16,2,4,16,128]{4,3,2,1,0:T(8,128)} %bitcast.4, f32[2,128]{1,0:T(2,128)} %diag_hbm.1, f32[2,4]{1,0:T(2,128)} %turn_hbm.1), custom_call_target="tpu_custom_call" | custom-call | tf_op jit(solution)/shard_map/pallas_call | solution.py:371
  118.3 1.3 %shard_map.47 = f32[2,16,2,4,16,128]{5,4,3,2,1,0:T(8,128)} custom-call(f32[2,16,2,4,16,128]{5,4,3,2,1,0:T(8,128)S(1)} %get-tuple-element.7.values, f32[8,128]{1,0:T(8,128)S(1)} %get-tuple-element.8.tangent), custom_call_target="tpu_custom_call" | custom-call | tf_op jit(solution)/shard_map/pallas_call | solution.py:399
where the time goes:
time: 121 us; the launch traced here: 120 us
  Pallas kernels  120 us (99%)
    pallas_call x1, Pallas kernels, body(): pl.pallas_call(functools.partial(kernel, nb, nl), out_shape=[pltpu.VMEM(h...  118 us

commit v1 on v0

--- a/solution.py
+++ b/solution.py
@@ -89,7 +89,7 @@
 def kernel(
     nb, nl, amp_hbm, en_hbm, diag_hbm, turn_hbm, out, last,
     amp, en, diag_ref, turn_ref, rs, re, back, table, slope, signed,
-    in_sem, s_send, s_recv, e_send, e_recv, b_send, b_recv,
+    in_sem, s_send, s_recv, e_send, e_recv, b_send, b_recv, side, outer_in, inner_in, here, all_in,
 ):
     _, blocks, groups, slabs, rows, lanes = amp.shape
     devices = nb * nl
@@ -108,41 +108,54 @@
     load_amp = pltpu.make_async_copy(amp_hbm, amp, in_sem.at[1])
     load_amp.start()
 
-    def peer(k):
-        db = xor(me_b, lax.rem(k, nb), nb)
-        dl = lax.rem(me_l + lax.div(k, nb), nl)
-        return db, dl
-
     flip_b = flips(me_b, nb)
     flip_l = flips(me_l, nl)
 
-    def to_peers_at_once(order, action):
-        for k in order:
-            db, dl = flip_b[k % nb], flip_l[k // nb]
-            action(db, dl, db * nl + dl)
-
-    def to_peers(action):
-        def step(k, carry):
-            db, dl = peer(k)
+    high, low = nl // 2, nl // 4
+    mirror = high + low
+    inner = lax.rem(lax.div(me_l, high), 2) != lax.rem(lax.div(me_l, low), 2)
+    sides = [(1 << place, 0) for place in range(bits_of(nb))]
+    sides += [(0, 1 << place) for place in range(bits_of(low))]
+    mirrored = devices // 4
+    unmirrored = others - mirrored
+
+    def signal(sem, flip):
+        pl.semaphore_signal(
+            sem, inc=1, device_id=(flip_b[flip[0]], flip_l[flip[1]]), device_id_type=MESH
+        )
+
+    def to_unmirrored(action):
+        def step(i, carry):
+            k = unmirrored - i
+            db, dl = xor(me_b, lax.rem(k, nb), nb), xor(me_l, lax.div(k, nb), nl)
             action(db, dl, db * nl + dl)
             return carry
 
-        lax.fori_loop(1, devices, step, 0)
+        lax.fori_loop(0, unmirrored, step, 0)
+
+    def to_peers(lane_flips, action):
+        for flip in lane_flips:
+            far_first = flip - low if flip & low else flip + low
+            mine = jnp.where(inner, far_first, flip) if flip & high else flip
+            dl = xor(me_l, mine, nl)
+
+            def step(i, carry):
+                db = xor(me_b, nb - 1 - i, nb)
+                action(db, dl, db * nl + dl)
+                return carry
+
+            lax.fori_loop(0, nb if flip else nb - 1, step, 0)
+
+    crossing_first = list(range(nl - 1, -1, -1))
+    in_turn = [flip for at in range(high - 1, -1, -1) for flip in (high + at, at)]
 
     barrier = pltpu.get_barrier_semaphore()
-    to_peers_at_once(
-        range(others, 0, -1),
-        lambda db, dl, d: pl.semaphore_signal(
-            barrier, inc=1, device_id=(db, dl), device_id_type=MESH
-        ),
-    )
-    pl.semaphore_wait(barrier, others)
-
-    def send_en(low, count, at, each=to_peers):
+
+    def send_en(low_slab, count, at, each):
         def one(db, dl, d):
             pltpu.make_async_remote_copy(
-                src_ref=en.at[lax.rem(d, blocks), lax.div(d, blocks), pl.ds(low, count)],
-                dst_ref=re.at[me, pl.ds(low, count)],
+                src_ref=en.at[lax.rem(d, blocks), lax.div(d, blocks), pl.ds(low_slab, count)],
+                dst_ref=re.at[me, pl.ds(low_slab, count)],
                 send_sem=e_send.at[at],
                 recv_sem=e_recv.at[at],
                 device_id=(db, dl),
@@ -150,6 +163,54 @@
             ).start()
 
         each(one)
+
+    def send_en_mirrored(found):
+        def each(action):
+            for bank_flip, lane_flip in found:
+                db, dl = flip_b[bank_flip], flip_l[lane_flip + mirror]
+                action(db, dl, db * nl + dl)
+
+        send_en(0, slabs, 2, each)
+
+    @pl.when(inner)
+    def _():
+        for flip in [(0, mirror)] + sides + [(0, low)]:
+            signal(barrier, flip)
+        pl.semaphore_wait(barrier, 1 + len(sides))
+        load_en.wait()
+        found = [(0, 0)]
+        send_en_mirrored(found)
+        for at, flip in enumerate(sides):
+            signal(side.at[at], flip)
+            pl.semaphore_wait(side.at[at], 1)
+            more = [(b + flip[0], l + flip[1]) for b, l in found]
+            send_en_mirrored(more)
+            found += more
+        pl.semaphore_wait(outer_in, 1)
+        signal(inner_in, (0, low))
+
+    @pl.when(jnp.logical_not(inner))
+    def _():
+        pl.semaphore_wait(barrier, 1)
+        signal(outer_in, (0, low))
+        load_en.wait()
+        pl.semaphore_wait(inner_in, 1)
+        for lane_flip in list(range(high, mirror)) + list(range(low, high)):
+            for bank_flip in range(nb):
+                signal(here, (bank_flip, lane_flip))
+
+    def meet_all():
+        @pl.when(inner)
+        def _():
+            pl.semaphore_wait(here, devices // 2)
+            signal(all_in, (0, low))
+
+        @pl.when(jnp.logical_not(inner))
+        def _():
+            pl.semaphore_wait(all_in, 1)
+            send_en_mirrored([(b, l) for l in range(low) for b in range(nb)])
+
+        send_en(0, 1, 0, to_unmirrored)
 
     def send_state(s):
         def one(db, dl, d):
@@ -162,7 +223,7 @@
                 device_id_type=MESH,
             ).start()
 
-        to_peers(one)
+        to_peers(crossing_first, one)
 
     def send_back(s):
         def one(db, dl, d):
@@ -175,18 +236,15 @@
                 device_id_type=MESH,
             ).start()
 
-        to_peers(one)
-
-    def wait_en(sem, low, count):
-        whole = re.at[pl.ds(0, others), pl.ds(low, count)]
+        to_peers(in_turn, one)
+
+    def wait_en(sem, peers, low_slab, count):
+        whole = re.at[pl.ds(0, peers), pl.ds(low_slab, count)]
         pltpu.make_async_copy(whole, whole, sem).wait()
 
     def wait_state(sem, s):
         whole = rs.at[pl.ds(0, others), :, s]
         pltpu.make_async_copy(whole, whole, sem).wait()
-
-    load_en.wait()
-    send_en(0, 1, 0, functools.partial(to_peers_at_once, range(1, devices)))
 
     load_turn.wait()
     load_diag.wait()
@@ -263,9 +321,11 @@
 
         over(blocks, phase_home)
         mix_home(amp, amp, 0, s)
+        if s == 0:
+            meet_all()
         send_state(s)
     if slabs > 1:
-        send_en(1, slabs - 1, 1)
+        send_en(1, slabs - 1, 1, to_unmirrored)
     for part in range(2):
         rs[me, part] = amp[part, my_block, my_group]
     re[me] = en[my_block, my_group]
@@ -327,9 +387,10 @@
     second_angle = jnp.broadcast_to(diag_ref[1:2, :], (rows, lanes))
     for s in range(slabs):
         if s == 0:
-            wait_en(e_recv.at[0], 0, 1)
+            wait_en(e_recv.at[2], mirrored, 0, slabs)
+            wait_en(e_recv.at[0], unmirrored, 0, 1)
         if s == 1:
-            wait_en(e_recv.at[1], 1, slabs - 1)
+            wait_en(e_recv.at[1], unmirrored, 1, slabs - 1)
 
         def phase_away(d):
             cosine, sine = cos_sin(second_angle * re[d, s])
@@ -348,9 +409,10 @@
         wait_state(b_recv.at[s], s)
         mix_home(back, out, 1, s)
 
-    wait_en(e_send.at[0], 0, 1)
+    wait_en(e_send.at[2], mirrored, 0, slabs)
+    wait_en(e_send.at[0], unmirrored, 0, 1)
     if slabs > 1:
-        wait_en(e_send.at[1], 1, slabs - 1)
+        wait_en(e_send.at[1], unmirrored, 1, slabs - 1)
     for s in range(slabs):
         wait_state(s_send.at[s], s)
         wait_state(b_send.at[s], s)
@@ -365,7 +427,7 @@
     home = (2, blocks, groups, slabs, rows, lanes)
     away = (devices, 2, slabs, rows, lanes)
     grant = VMEM_MOST - 4 * amplitudes.size - ROOM
-    dma = pltpu.SemaphoreType.DMA
+    dma, regular = pltpu.SemaphoreType.DMA, pltpu.SemaphoreType.REGULAR
     hbm = pl.BlockSpec(memory_space=pl.ANY)
     vmem = pl.BlockSpec(memory_space=pltpu.VMEM)
     values, tangent = pl.pallas_call(
@@ -387,10 +449,15 @@
             dma((4,)),
             dma((slabs,)),
             dma((slabs,)),
-            dma((2,)),
-            dma((2,)),
+            dma((3,)),
+            dma((3,)),
             dma((slabs,)),
             dma((slabs,)),
+            regular((bits_of(devices) - 2,)),
+            regular,
+            regular,
+            regular,
+            regular,
         ],
         compiler_params=pltpu.CompilerParams(
             collective_id=0, has_side_effects=True, vmem_limit_bytes=grant

time: 121 us -> 119 us (0.983)
  no operation moved by 1% of the time
where the time goes in v1:
time: 119 us
  Pallas kernels  119 us (100%)
    pallas_call x1, Pallas kernels, body(): pl.pallas_call(functools.partial(kernel, nb, nl), out_shape=[pltpu.VMEM(h...  117 us

profile of v1, /device:TPU:9, one launch (start us, length us, event | category | flops | bytes accessed | tf_op | source)
XLA Modules:
  0.0 118.7 jit_solution(6618588555880650937)
XLA Ops:
  0.0 117.4 %shard_map.46 = (f32[2,16,2,4,16,128]{5,4,3,2,1,0:T(8,128)S(1)}, f32[8,128]{1,0:T(8,128)S(1)}) custom-call(f32[2,16,2,4,16,128]{5,4,3,2,1,0:T(8,128)} %bitcast.3, f32[16,2,4,16,128]{4,3,2,1,0:T(8,128)} %bitcast.4, f32[2,128]{1,0:T(2,128)} %diag_hbm.1, f32[2,4]{1,0:T(2,128)} %turn_hbm.1), custom_call_target="tpu_custom_call" | custom-call | tf_op jit(solution)/shard_map/pallas_call | solution.py:433
  117.4 1.3 %shard_map.47 = f32[2,16,2,4,16,128]{5,4,3,2,1,0:T(8,128)} custom-call(f32[2,16,2,4,16,128]{5,4,3,2,1,0:T(8,128)S(1)} %get-tuple-element.7.values, f32[8,128]{1,0:T(8,128)S(1)} %get-tuple-element.8.tangent), custom_call_target="tpu_custom_call" | custom-call | tf_op jit(solution)/shard_map/pallas_call | solution.py:466

commit v2 on v1

--- a/solution.py
+++ b/solution.py
@@ -99,6 +99,55 @@
     me = me_b * nl + me_l
     my_block, my_group = lax.rem(me, blocks), lax.div(me, blocks)
 
+    flip_b = flips(me_b, nb)
+    flip_l = flips(me_l, nl)
+
+    high, low = nl // 2, nl // 4
+    mirror = high + low
+    inner = lax.rem(lax.div(me_l, high), 2) != lax.rem(lax.div(me_l, low), 2)
+    sides = [(1 << place, 0) for place in range(1, bits_of(nb))]
+    sides += [(0, 1 << place) for place in range(bits_of(low))]
+    mirrored = devices // 4
+    unmirrored = others - mirrored
+
+    def signal(sem, flip):
+        pl.semaphore_signal(
+            sem, inc=1, device_id=(flip_b[flip[0]], flip_l[flip[1]]), device_id_type=MESH
+        )
+
+    def to_unmirrored(action):
+        def step(i, carry):
+            k = unmirrored - i
+            db, dl = xor(me_b, lax.rem(k, nb), nb), xor(me_l, lax.div(k, nb), nl)
+            action(db, dl, db * nl + dl)
+            return carry
+
+        lax.fori_loop(0, unmirrored, step, 0)
+
+    def to_peers(lane_flips, action):
+        for flip in lane_flips:
+            far_first = flip - low if flip & low else flip + low
+            mine = jnp.where(inner, far_first, flip) if flip & high else flip
+            dl = xor(me_l, mine, nl)
+
+            def step(i, carry):
+                db = xor(me_b, nb - 1 - i, nb)
+                action(db, dl, db * nl + dl)
+                return carry
+
+            lax.fori_loop(0, nb if flip else nb - 1, step, 0)
+
+    crossing_first = list(range(nl - 1, -1, -1))
+    in_turn = [flip for at in range(high - 1, -1, -1) for flip in (high + at, at)]
+    crossing_last = [flip for at in range(high - 1, -1, -1) for flip in (at, high + at)]
+
+    barrier = pltpu.get_barrier_semaphore()
+
+    @pl.when(inner)
+    def _():
+        for flip in [(0, mirror), (1, mirror)] + sides + [(1, 0), (0, low)]:
+            signal(barrier, flip)
+
     load_en = pltpu.make_async_copy(en_hbm, en, in_sem.at[0])
     load_en.start()
     load_turn = pltpu.make_async_copy(turn_hbm, turn_ref, in_sem.at[2])
@@ -107,49 +156,6 @@
     load_diag.start()
     load_amp = pltpu.make_async_copy(amp_hbm, amp, in_sem.at[1])
     load_amp.start()
-
-    flip_b = flips(me_b, nb)
-    flip_l = flips(me_l, nl)
-
-    high, low = nl // 2, nl // 4
-    mirror = high + low
-    inner = lax.rem(lax.div(me_l, high), 2) != lax.rem(lax.div(me_l, low), 2)
-    sides = [(1 << place, 0) for place in range(bits_of(nb))]
-    sides += [(0, 1 << place) for place in range(bits_of(low))]
-    mirrored = devices // 4
-    unmirrored = others - mirrored
-
-    def signal(sem, flip):
-        pl.semaphore_signal(
-            sem, inc=1, device_id=(flip_b[flip[0]], flip_l[flip[1]]), device_id_type=MESH
-        )
-
-    def to_unmirrored(action):
-        def step(i, carry):
-            k = unmirrored - i
-            db, dl = xor(me_b, lax.rem(k, nb), nb), xor(me_l, lax.div(k, nb), nl)
-            action(db, dl, db * nl + dl)
-            return carry
-
-        lax.fori_loop(0, unmirrored, step, 0)
-
-    def to_peers(lane_flips, action):
-        for flip in lane_flips:
-            far_first = flip - low if flip & low else flip + low
-            mine = jnp.where(inner, far_first, flip) if flip & high else flip
-            dl = xor(me_l, mine, nl)
-
-            def step(i, carry):
-                db = xor(me_b, nb - 1 - i, nb)
-                action(db, dl, db * nl + dl)
-                return carry
-
-            lax.fori_loop(0, nb if flip else nb - 1, step, 0)
-
-    crossing_first = list(range(nl - 1, -1, -1))
-    in_turn = [flip for at in range(high - 1, -1, -1) for flip in (high + at, at)]
-
-    barrier = pltpu.get_barrier_semaphore()
 
     def send_en(low_slab, count, at, each):
         def one(db, dl, d):
@@ -174,11 +180,9 @@
 
     @pl.when(inner)
     def _():
-        for flip in [(0, mirror)] + sides + [(0, low)]:
-            signal(barrier, flip)
-        pl.semaphore_wait(barrier, 1 + len(sides))
+        pl.semaphore_wait(barrier, 3 + len(sides))
         load_en.wait()
-        found = [(0, 0)]
+        found = [(0, 0), (1, 0)]
         send_en_mirrored(found)
         for at, flip in enumerate(sides):
             signal(side.at[at], flip)
@@ -223,7 +227,7 @@
                 device_id_type=MESH,
             ).start()
 
-        to_peers(crossing_first, one)
+        to_peers(in_turn, one)
 
     def send_back(s):
         def one(db, dl, d):
@@ -236,7 +240,7 @@
                 device_id_type=MESH,
             ).start()
 
-        to_peers(in_turn, one)
+        to_peers(crossing_last if s == slabs - 1 else crossing_first, one)
 
     def wait_en(sem, peers, low_slab, count):
         whole = re.at[pl.ds(0, peers), pl.ds(low_slab, count)]
@@ -453,7 +457,7 @@
             dma((3,)),
             dma((slabs,)),
             dma((slabs,)),
-            regular((bits_of(devices) - 2,)),
+            regular((bits_of(nb) + bits_of(nl) - 3,)),
             regular,
             regular,
             regular,

time: 119 us -> 119 us (level)
  no operation moved by 1% of the time
where the time goes in v2:
time: 119 us; the launch traced here: 118 us
  Pallas kernels  118 us (99%)
    pallas_call x1, Pallas kernels, body(): pl.pallas_call(functools.partial(kernel, nb, nl), out_shape=[pltpu.VMEM(h...  117 us

profile of v2, /device:TPU:9, one launch (start us, length us, event | category | flops | bytes accessed | tf_op | source)
XLA Modules:
  0.0 118.4 jit_solution(14900307824425290823)
XLA Ops:
  0.0 117.1 %shard_map.46 = (f32[2,16,2,4,16,128]{5,4,3,2,1,0:T(8,128)S(1)}, f32[8,128]{1,0:T(8,128)S(1)}) custom-call(f32[2,16,2,4,16,128]{5,4,3,2,1,0:T(8,128)} %bitcast.3, f32[16,2,4,16,128]{4,3,2,1,0:T(8,128)} %bitcast.4, f32[2,128]{1,0:T(2,128)} %diag_hbm.1, f32[2,4]{1,0:T(2,128)} %turn_hbm.1), custom_call_target="tpu_custom_call" | custom-call | tf_op jit(solution)/shard_map/pallas_call | solution.py:437
  117.1 1.3 %shard_map.47 = f32[2,16,2,4,16,128]{5,4,3,2,1,0:T(8,128)} custom-call(f32[2,16,2,4,16,128]{5,4,3,2,1,0:T(8,128)S(1)} %get-tuple-element.7.values, f32[8,128]{1,0:T(8,128)S(1)} %get-tuple-element.8.tangent), custom_call_target="tpu_custom_call" | custom-call | tf_op jit(solution)/shard_map/pallas_call | solution.py:470

commit v3 on v2

--- a/solution.py
+++ b/solution.py
@@ -90,6 +90,7 @@
     nb, nl, amp_hbm, en_hbm, diag_hbm, turn_hbm, out, last,
     amp, en, diag_ref, turn_ref, rs, re, back, table, slope, signed,
     in_sem, s_send, s_recv, e_send, e_recv, b_send, b_recv, side, outer_in, inner_in, here, all_in,
+    en_first, told,
 ):
     _, blocks, groups, slabs, rows, lanes = amp.shape
     devices = nb * nl
@@ -115,14 +116,17 @@
             sem, inc=1, device_id=(flip_b[flip[0]], flip_l[flip[1]]), device_id_type=MESH
         )
 
-    def to_unmirrored(action):
+    def to_last(last, count, action):
         def step(i, carry):
-            k = unmirrored - i
+            k = last - i
             db, dl = xor(me_b, lax.rem(k, nb), nb), xor(me_l, lax.div(k, nb), nl)
             action(db, dl, db * nl + dl)
             return carry
 
-        lax.fori_loop(0, unmirrored, step, 0)
+        lax.fori_loop(0, count, step, 0)
+
+    to_mirrored = functools.partial(to_last, others, mirrored)
+    to_unmirrored = functools.partial(to_last, unmirrored, unmirrored)
 
     def to_peers(lane_flips, action):
         for flip in lane_flips:
@@ -143,10 +147,31 @@
 
     barrier = pltpu.get_barrier_semaphore()
 
+    upper = jnp.logical_and(inner, lax.div(me_l, high) == 1)
+    lower = jnp.logical_and(inner, lax.div(me_l, high) == 0)
+    facing = [(0, mirror), (1, mirror)]
+
     @pl.when(inner)
     def _():
-        for flip in [(0, mirror), (1, mirror)] + sides + [(1, 0), (0, low)]:
+        for flip in facing:
             signal(barrier, flip)
+
+    @pl.when(lower)
+    def _():
+        for flip in sides + [(1, 0)]:
+            signal(barrier, flip)
+
+    def index_of(flip):
+        return flip_b[flip[0]] * nl + flip_l[flip[1]]
+
+    @pl.when(inner)
+    def _():
+        signal(barrier, (0, low))
+        for at, flip in enumerate(facing):
+            d = index_of(flip)
+            pltpu.make_async_copy(
+                en_hbm.at[lax.rem(d, blocks), lax.div(d, blocks)], en_first.at[at], in_sem.at[4]
+            ).start()
 
     load_en = pltpu.make_async_copy(en_hbm, en, in_sem.at[0])
     load_en.start()
@@ -178,18 +203,50 @@
 
         send_en(0, slabs, 2, each)
 
-    @pl.when(inner)
+    def send_first():
+        pltpu.make_async_copy(en_first, en_first, in_sem.at[4]).wait()
+        for at, flip in enumerate(facing):
+            pltpu.make_async_remote_copy(
+                src_ref=en_first.at[at],
+                dst_ref=re.at[me],
+                send_sem=e_send.at[2],
+                recv_sem=e_recv.at[2],
+                device_id=(flip_b[flip[0]], flip_l[flip[1]]),
+                device_id_type=MESH,
+            ).start()
+
+    near = [(0, 0), (1, 0)]
+    single = [(b + flip[0], flip[1]) for flip in sides for b in range(2)]
+    every = [(b, l) for l in range(low) for b in range(nb)]
+
+    @pl.when(lower)
     def _():
         pl.semaphore_wait(barrier, 3 + len(sides))
+        send_first()
+        for flip in facing:
+            signal(told.at[0], flip)
         load_en.wait()
-        found = [(0, 0), (1, 0)]
-        send_en_mirrored(found)
+        found = list(near)
         for at, flip in enumerate(sides):
             signal(side.at[at], flip)
             pl.semaphore_wait(side.at[at], 1)
             more = [(b + flip[0], l + flip[1]) for b, l in found]
             send_en_mirrored(more)
             found += more
+        signal(told.at[1], (0, mirror))
+
+    @pl.when(upper)
+    def _():
+        pl.semaphore_wait(barrier, 2)
+        send_first()
+        load_en.wait()
+        pl.semaphore_wait(told.at[0], 2)
+        send_en_mirrored(single)
+        pl.semaphore_wait(told.at[1], 1)
+        send_en_mirrored([flip for flip in every if flip not in near + single])
+
+    @pl.when(inner)
+    def _():
         pl.semaphore_wait(outer_in, 1)
         signal(inner_in, (0, low))
 
@@ -206,17 +263,20 @@
     def meet_all():
         @pl.when(inner)
         def _():
+            send_state(0, to_mirrored)
             pl.semaphore_wait(here, devices // 2)
             signal(all_in, (0, low))
 
         @pl.when(jnp.logical_not(inner))
         def _():
             pl.semaphore_wait(all_in, 1)
-            send_en_mirrored([(b, l) for l in range(low) for b in range(nb)])
+            send_state(0, to_mirrored)
+            send_en_mirrored(every)
 
         send_en(0, 1, 0, to_unmirrored)
-
-    def send_state(s):
+        send_state(0, to_unmirrored)
+
+    def send_state(s, each):
         def one(db, dl, d):
             pltpu.make_async_remote_copy(
                 src_ref=amp.at[:, lax.rem(d, blocks), lax.div(d, blocks), s],
@@ -227,7 +287,7 @@
                 device_id_type=MESH,
             ).start()
 
-        to_peers(in_turn, one)
+        each(one)
 
     def send_back(s):
         def one(db, dl, d):
@@ -327,7 +387,8 @@
         mix_home(amp, amp, 0, s)
         if s == 0:
             meet_all()
-        send_state(s)
+        else:
+            send_state(s, functools.partial(to_peers, in_turn))
     if slabs > 1:
         send_en(1, slabs - 1, 1, to_unmirrored)
     for part in range(2):
@@ -410,16 +471,18 @@
         back[part, my_block, my_group] = rs[me, part]
 
     for s in range(slabs):
+        if s == slabs - 1:
+            wait_en(e_send.at[2], mirrored, 0, slabs)
+            wait_en(e_send.at[0], unmirrored, 0, 1)
+            if slabs > 1:
+                wait_en(e_send.at[1], unmirrored, 1, slabs - 1)
+            for before in range(slabs):
+                wait_state(s_send.at[before], before)
+            for before in range(slabs - 1):
+                wait_state(b_send.at[before], before)
         wait_state(b_recv.at[s], s)
         mix_home(back, out, 1, s)
-
-    wait_en(e_send.at[2], mirrored, 0, slabs)
-    wait_en(e_send.at[0], unmirrored, 0, 1)
-    if slabs > 1:
-        wait_en(e_send.at[1], unmirrored, 1, slabs - 1)
-    for s in range(slabs):
-        wait_state(s_send.at[s], s)
-        wait_state(b_send.at[s], s)
+    wait_state(b_send.at[slabs - 1], slabs - 1)
 
 
 def body(nb, nl, amplitudes, energies, diagonal_angles, turn_angles):
@@ -450,7 +513,7 @@
             pltpu.VMEM((LAYERS, 2 * lanes, 2 * lanes), jnp.bfloat16),
             pltpu.VMEM((LAYERS, 4, SUB, lanes), jnp.float32),
             pltpu.VMEM((LAYERS, 3, SUB, lanes), jnp.float32),
-            dma((4,)),
+            dma((5,)),
             dma((slabs,)),
             dma((slabs,)),
             dma((3,)),
@@ -462,6 +525,8 @@
             regular,
             regular,
             regular,
+            pltpu.VMEM((2,) + away[2:], jnp.float32),
+            regular((2,)),
         ],
         compiler_params=pltpu.CompilerParams(
             collective_id=0, has_side_effects=True, vmem_limit_bytes=grant

time: 119 us -> 118 us (level)
  no operation moved by 1% of the time
where the time goes in v3:
time: 118 us
  Pallas kernels  118 us (100%)
    pallas_call x1, Pallas kernels, body(): pl.pallas_call(functools.partial(kernel, nb, nl), out_shape=[pltpu.VMEM(h...  117 us

profile of v3, /device:TPU:9, one launch (start us, length us, event | category | flops | bytes accessed | tf_op | source)
XLA Modules:
  0.0 118.0 jit_solution(16327606014675814339)
XLA Ops:
  0.0 116.7 %shard_map.46 = (f32[2,16,2,4,16,128]{5,4,3,2,1,0:T(8,128)S(1)}, f32[8,128]{1,0:T(8,128)S(1)}) custom-call(f32[2,16,2,4,16,128]{5,4,3,2,1,0:T(8,128)} %bitcast.3, f32[16,2,4,16,128]{4,3,2,1,0:T(8,128)} %bitcast.4, f32[2,128]{1,0:T(2,128)} %diag_hbm.1, f32[2,4]{1,0:T(2,128)} %turn_hbm.1), custom_call_target="tpu_custom_call" | custom-call | tf_op jit(solution)/shard_map/pallas_call | solution.py:500
  116.7 1.3 %shard_map.47 = f32[2,16,2,4,16,128]{5,4,3,2,1,0:T(8,128)} custom-call(f32[2,16,2,4,16,128]{5,4,3,2,1,0:T(8,128)S(1)} %get-tuple-element.7.values, f32[8,128]{1,0:T(8,128)S(1)} %get-tuple-element.8.tangent), custom_call_target="tpu_custom_call" | custom-call | tf_op jit(solution)/shard_map/pallas_call | solution.py:535

commit v4 on v3

--- a/solution.py
+++ b/solution.py
@@ -167,6 +167,9 @@
     @pl.when(inner)
     def _():
         signal(barrier, (0, low))
+
+    @pl.when(upper)
+    def _():
         for at, flip in enumerate(facing):
             d = index_of(flip)
             pltpu.make_async_copy(
@@ -222,10 +225,10 @@
     @pl.when(lower)
     def _():
         pl.semaphore_wait(barrier, 3 + len(sides))
-        send_first()
         for flip in facing:
             signal(told.at[0], flip)
         load_en.wait()
+        send_en_mirrored(near)
         found = list(near)
         for at, flip in enumerate(sides):
             signal(side.at[at], flip)
@@ -270,11 +273,11 @@
         @pl.when(jnp.logical_not(inner))
         def _():
             pl.semaphore_wait(all_in, 1)
+            send_en_mirrored(every)
             send_state(0, to_mirrored)
-            send_en_mirrored(every)
-
+
+        send_state(0, to_unmirrored)
         send_en(0, 1, 0, to_unmirrored)
-        send_state(0, to_unmirrored)
 
     def send_state(s, each):
         def one(db, dl, d):

time: 118 us -> 118 us (level)
  no operation moved by 1% of the time
where the time goes in v4:
time: 118 us
  Pallas kernels  118 us (100%)
    pallas_call x1, Pallas kernels, body(): pl.pallas_call(functools.partial(kernel, nb, nl), out_shape=[pltpu.VMEM(h...  117 us

profile of v4, /device:TPU:9, one launch (start us, length us, event | category | flops | bytes accessed | tf_op | source)
XLA Modules:
  0.0 118.0 jit_solution(6732413152880064672)
XLA Ops:
  0.0 116.6 %shard_map.46 = (f32[2,16,2,4,16,128]{5,4,3,2,1,0:T(8,128)S(1)}, f32[8,128]{1,0:T(8,128)S(1)}) custom-call(f32[2,16,2,4,16,128]{5,4,3,2,1,0:T(8,128)} %bitcast.3, f32[16,2,4,16,128]{4,3,2,1,0:T(8,128)} %bitcast.4, f32[2,128]{1,0:T(2,128)} %diag_hbm.1, f32[2,4]{1,0:T(2,128)} %turn_hbm.1), custom_call_target="tpu_custom_call" | custom-call | tf_op jit(solution)/shard_map/pallas_call | solution.py:503
  116.6 1.3 %shard_map.47 = f32[2,16,2,4,16,128]{5,4,3,2,1,0:T(8,128)} custom-call(f32[2,16,2,4,16,128]{5,4,3,2,1,0:T(8,128)S(1)} %get-tuple-element.7.values, f32[8,128]{1,0:T(8,128)S(1)} %get-tuple-element.8.tangent), custom_call_target="tpu_custom_call" | custom-call | tf_op jit(solution)/shard_map/pallas_call | solution.py:538

commit v5 on v4

--- a/solution.py
+++ b/solution.py
@@ -143,7 +143,12 @@
 
     crossing_first = list(range(nl - 1, -1, -1))
     in_turn = [flip for at in range(high - 1, -1, -1) for flip in (high + at, at)]
-    crossing_last = [flip for at in range(high - 1, -1, -1) for flip in (at, high + at)]
+    crossing_last = [
+        side_flip + at - low_flip
+        for at in range(high - 1, -1, -2)
+        for side_flip in (0, high)
+        for low_flip in (0, 1)
+    ]
 
     barrier = pltpu.get_barrier_semaphore()
 

time: 118 us -> 118 us (level)
  no operation moved by 1% of the time
where the time goes in v5:
time: 118 us
  Pallas kernels  118 us (100%)
    pallas_call x1, Pallas kernels, body(): pl.pallas_call(functools.partial(kernel, nb, nl), out_shape=[pltpu.VMEM(h...  117 us

profile of v5, /device:TPU:9, one launch (start us, length us, event | category | flops | bytes accessed | tf_op | source)
XLA Modules:
  0.0 118.0 jit_solution(8597893992166732675)
XLA Ops:
  0.0 116.6 %shard_map.46 = (f32[2,16,2,4,16,128]{5,4,3,2,1,0:T(8,128)S(1)}, f32[8,128]{1,0:T(8,128)S(1)}) custom-call(f32[2,16,2,4,16,128]{5,4,3,2,1,0:T(8,128)} %bitcast.3, f32[16,2,4,16,128]{4,3,2,1,0:T(8,128)} %bitcast.4, f32[2,128]{1,0:T(2,128)} %diag_hbm.1, f32[2,4]{1,0:T(2,128)} %turn_hbm.1), custom_call_target="tpu_custom_call" | custom-call | tf_op jit(solution)/shard_map/pallas_call | solution.py:508
  116.6 1.3 %shard_map.47 = f32[2,16,2,4,16,128]{5,4,3,2,1,0:T(8,128)} custom-call(f32[2,16,2,4,16,128]{5,4,3,2,1,0:T(8,128)S(1)} %get-tuple-element.7.values, f32[8,128]{1,0:T(8,128)S(1)} %get-tuple-element.8.tangent), custom_call_target="tpu_custom_call" | custom-call | tf_op jit(solution)/shard_map/pallas_call | solution.py:543
